TPU v7x, 32 devices: a whole 2x2x4 slice. The times are simulated.
32 devices in a mesh: dp: 4 (over y, x), row: 4 (over z), col: 2 (over core).
Axes of the slice: x: 2, y: 2, z: 4, core: 2. Of those that a mesh axis runs over, the one named last changes fastest.
Arguments:
- activations: bfloat16 [4, 64, 128, 512], P('dp', None, 'row', 'col'), may hold values from -18 to 18
- kernel: bfloat16 [3, 3, 64, 64], replicated, may hold values from -0.125 to 0.125
- gain: float32 [64], replicated, may hold values from 0.25 to 1.75
- cotangent: bfloat16 [4, 64, 128, 512], P('dp', None, 'row', 'col'), may hold values from -16 to 16
Outputs:
- input_grad: bfloat16 [4, 64, 128, 512], P('dp', None, 'row', 'col')
- weight_grad: float32 [3, 3, 64, 64], P(None, None, 'dp')
- gain_grad: float32 [64], replicated
- shift_grad: float32 [64], replicated
All inputs are finite; a program needn't handle non-finite values.
Results may differ from a plain program's by a relative error of at most 0.0049.
Values may be sent and summed in bfloat16 or wider, within the bound.
A program may use at most 64 MiB of HBM per device.

v0:
```python
import jax
import jax.numpy as jnp
from jax import lax
from jax.sharding import PartitionSpec as P


def with_halo(shard, sides, width):
    for axis, dim in sides:
        count, length = (lax.axis_size(axis), shard.shape[dim])
        up = [(i, (i + 1) % count) for i in range(count - 1)]
        down = [(j, i) for i, j in up]
        last = lax.slice_in_dim(shard, length - width, length, axis=dim)
        initial = lax.slice_in_dim(shard, 0, width, axis=dim)
        before = lax.ppermute(last, axis, up)
        after = lax.ppermute(initial, axis, down)
        shard = jnp.concatenate([before, shard, after], axis=dim)
    return shard


def per_device(activations, kernel, gain, cotangent):
    images, channels, height, width = activations.shape
    total = jnp.float32(
        images * height * width * lax.axis_size("dp") * lax.axis_size("row") * lax.axis_size("col")
    )
    padded = with_halo(activations, (("row", 2), ("col", 3)), 1)
    pre = jnp.zeros((images, channels, height, width), jnp.float32)
    for tap_row in range(3):
        for tap_col in range(3):
            window = padded[:, :, tap_row : tap_row + height, tap_col : tap_col + width]
            pre = pre + jnp.einsum(
                "oc,bchw->bohw",
                kernel[tap_row, tap_col],
                window,
                preferred_element_type=jnp.float32,
            )
    grad = cotangent.astype(jnp.float32)
    local_pre = jnp.sum(pre, axis=(0, 2, 3))
    local_sq = jnp.sum(pre * pre, axis=(0, 2, 3))
    local_cot = jnp.sum(grad, axis=(0, 2, 3))
    local_cross = jnp.sum(grad * pre, axis=(0, 2, 3))
    sum_pre, sum_sq, sum_cot, sum_cross = lax.psum(
        (local_pre, local_sq, local_cot, local_cross), ("dp", "row", "col")
    )
    mean = sum_pre / total
    rstd = lax.rsqrt(sum_sq / total - mean * mean + 1e-05)
    sum_norm = (sum_cross - mean * sum_cot) * rstd
    normed = (pre - mean[:, None, None]) * rstd[:, None, None]
    pre_grad = (gain * rstd)[:, None, None] * (
        grad - (sum_cot / total)[:, None, None] - normed * (sum_norm / total)[:, None, None]
    )
    pre_grad = pre_grad.astype(jnp.bfloat16)
    grad_padded = with_halo(pre_grad, (("row", 2), ("col", 3)), 1)
    input_grad = jnp.zeros((images, channels, height, width), jnp.float32)
    kernel_terms = []
    for tap_row in range(3):
        for tap_col in range(3):
            shifted = grad_padded[
                :, :, 2 - tap_row : 2 - tap_row + height, 2 - tap_col : 2 - tap_col + width
            ]
            input_grad = input_grad + jnp.einsum(
                "oc,bohw->bchw",
                kernel[tap_row, tap_col],
                shifted,
                preferred_element_type=jnp.float32,
            )
            window = padded[:, :, tap_row : tap_row + height, tap_col : tap_col + width]
            kernel_terms.append(
                jnp.einsum("bohw,bchw->oc", pre_grad, window, preferred_element_type=jnp.float32)
            )
    factor = total ** (-0.5)
    local_kernel = jnp.stack(kernel_terms).reshape(3, 3, channels, channels) * factor
    spatial = lax.psum(local_kernel, ("row", "col"))
    weight_grad = lax.psum_scatter(spatial, "dp", scatter_dimension=2, tiled=True)
    return (input_grad.astype(jnp.bfloat16), weight_grad, sum_norm / total, sum_cot / total)


def solution(mesh):
    return jax.shard_map(
        per_device,
        mesh=mesh,
        in_specs=(P("dp", None, "row", "col"), P(), P(), P("dp", None, "row", "col")),
        out_specs=(P("dp", None, "row", "col"), P(None, None, "dp", None), P(), P()),
        check_vma=False,
    )
```

profile of v0, /device:TPU:0, one launch (start us, length us, event | category | flops | bytes accessed | tf_op | source)
XLA Modules:
  0.0 162.4 jit_solution(4085869104326707929)
XLA Ops:
  7.2 1.9 %copy.26 = bf16[1,64,32,256]{3,1,2,0:T(8,128)(2,1)S(1)} copy(bf16[1,64,32,256]{3,2,1,0:T(8,128)(2,1)} %param.4) | data formatting | bytes 2097152 | tf_op args[0]
  9.2 5.0 %collective-permute-start = (bf16[1,64,1,256]{3,1,2,0:T(8,128)(2,1)S(1)}, bf16[1,64,1,256]{3,1,2,0:T(8,128)(2,1)S(1)}, u32[]{:S(2)}, u32[]{:S(2)}) collective-permute-start(bf16[1,64,1,256]{3,1,2,0:T(8,128)(2,1)S(1)} %get-tuple-element.29), channel_id=1, source_target_pairs={{0,2},{2,4},{4,6},{1,3},{3,5},{5,7},{8,10},{10,12},{12,14},{9,11},... | collective-permute-start | bytes 98312 | tf_op jit(solution)/shard_map/ppermute | solution.py:14
  14.1 1.3 collective-permute-start.1
  15.4 2.2 %fusion.55 = f32[32,256,64]{1,2,0:T(8,128)} fusion(bf16[64,32,256]{2,1,0:T(8,128)(2,1)S(1)} %bitcast.222, bf16[3,3,64,64]{3,2,1,0:T(8,128)(2,1)S(1)} %copy-done.18), kind=kOutput, calls=%fused_computation.92 | convolution fusion | flops 67108864 | bytes 3162112 | tf_op jit(solution)/shard_map/oc,bchw->bohw/dot_general | solution.py:30
  18.3 1.7 %collective-permute-done.1 = bf16[1,64,1,256]{3,1,2,0:T(8,128)(2,1)S(1)} collective-permute-done((bf16[1,64,1,256]{3,1,2,0:T(8,128)(2,1)S(1)}, bf16[1,64,1,256]{3,1,2,0:T(8,128)(2,1)S(1)}, u32[]{:S(2)}, u32[]{:S(2)}) %collective-permute-start.1) | collective-permute-done | bytes 32800 | tf_op jit(solution)/shard_map/ppermute | solution.py:15
  22.2 3.0 %collective-permute-start.2 = (bf16[1,64,34,1]{1,2,3,0:T(8,128)(2,1)S(1)}, bf16[1,64,34,1]{1,2,3,0:T(8,128)(2,1)S(1)}, u32[]{:S(2)}, u32[]{:S(2)}) collective-permute-start(bf16[1,64,34,1]{1,2,3,0:T(8,128)(2,1)S(1)} %copy.29), channel_id=1, source_target_pairs={{0,1},{2,3},{4,5},{6,7},{8,9},{10,11},{12,13},{14,15},{16,17},{18,... | collective-permute-start | bytes 13064 | tf_op jit(solution)/shard_map/ppermute | solution.py:14
  25.2 1.8 %fusion.58 = f32[32,256,64]{1,2,0:T(8,128)} fusion(bf16[1,64,32,256]{3,1,2,0:T(8,128)(2,1)S(1)} %copy.26, bf16[1,64,1,256]{3,1,2,0:T(8,128)(2,1)S(1)} %collective-permute-done, bf16[3,3,64,64]{3,2,1,0:T(8,128)(2,1)S(1)} %copy-done.18), kind=kOutput, calls=%fused_computation.94 | convolution fusion | flops 69206016 | bytes 3194880 | tf_op jit(solution)/shard_map/oc,bchw->bohw/dot_general | solution.py:30
  27.0 1.7 %fusion.61 = f32[32,256,64]{1,2,0:T(8,128)} fusion(bf16[1,64,1,256]{3,1,2,0:T(8,128)(2,1)S(1)} %collective-permute-done.1, bf16[1,64,32,256]{3,1,2,0:T(8,128)(2,1)S(1)} %copy.26, bf16[3,3,64,64]{3,2,1,0:T(8,128)(2,1)S(1)} %copy-done.18), kind=kOutput, calls=%fused_computation.95 | convolution fusion | flops 69206016 | bytes 3194880 | tf_op jit(solution)/shard_map/oc,bchw->bohw/dot_general | solution.py:30
  29.1 2.1 %fusion.78 = f32[32,256,64]{1,2,0:T(8,128)} fusion(bf16[3,3,64,64]{3,2,1,0:T(8,128)(2,1)S(1)} %copy-done.18, bf16[1,64,34,256]{3,1,2,0:T(8,128)(2,1)S(1)} %constant_dynamic-update-slice_fusion, bf16[1,64,34,1]{3,1,2,0:T(8,128)(2,1)S(1)} %copy.33), kind=kOutput, calls=%fused_computation.109 | convolution fusion | flops 69206016 | bytes 3784704 | tf_op jit(solution)/shard_map/oc,bchw->bohw/dot_general | solution.py:30
  31.1 2.1 %fusion.86 = f32[32,256,64]{1,2,0:T(8,128)} fusion(bf16[3,3,64,64]{3,2,1,0:T(8,128)(2,1)S(1)} %copy-done.18, bf16[1,64,34,256]{3,1,2,0:T(8,128)(2,1)S(1)} %constant_dynamic-update-slice_fusion, bf16[1,64,34,1]{3,1,2,0:T(8,128)(2,1)S(1)} %copy.33), kind=kOutput, calls=%fused_computation.117 | convolution fusion | flops 69206016 | bytes 3784704 | tf_op jit(solution)/shard_map/oc,bchw->bohw/dot_general | solution.py:30
  38.3 3.8 %fusion.3 = (f32[64]{0:T(128)S(1)}, f32[64]{0:T(128)S(1)}, f32[64]{0:T(128)S(1)}, f32[32,256,64]{1,2,0:T(8,128)S(1)}) fusion(bf16[1,64,32,256]{3,2,1,0:T(8,128)(2,1)} %param.7, bf16[1,64,34,1]{3,1,2,0:T(8,128)(2,1)S(1)} %copy-done.2, bf16[1,64,34,256]{3,1,2,0:T(8,128)(2,1)S(1)} %constant_dynamic-update-slice_fusion, ...), kind=kOutput, calls=%fused_computation.6 | convolution fusion | flops 76545856 | bytes 21611264 | tf_op jit(solution)/shard_map/oc,bchw->bohw/dot_general | solution.py:30
  42.3 40.6 %all-reduce = (f32[64]{0:T(128)S(1)}, f32[64]{0:T(128)S(1)}, f32[64]{0:T(128)S(1)}, f32[64]{0:T(128)S(1)}) all-reduce(f32[64]{0:T(128)S(1)} %get-tuple-element.13, f32[64]{0:T(128)S(1)} %reduce_sum.37, f32[64]{0:T(128)S(1)} %get-tuple-element.12, f32[64]{0:T(128)S(1)} %get-tuple-element.14), channel_id=1, replica_groups=mesh['dp'=4,'row'=4,'col'=2] {'dp','row','col'}, use_global_device_ids=true, to_apply=%region_1.0 | all-reduce | flops 256 | bytes 2048 | tf_op jit(solution)/shard_map/psum | solution.py:41
  83.0 2.8 %fusion.2 = bf16[1,64,32,256]{3,1,2,0:T(8,128)(2,1)S(1)} fusion(f32[32,256,64]{1,2,0:T(8,128)} %copy-done, f32[64]{0:T(128)S(1)} %get-tuple-element.32, f32[64]{0:T(128)S(1)} %get-tuple-element.20, f32[64]{0:T(128)S(1)} %get-tuple-element.33, f32[64]{0:T(128)S(1)} %get-tuple-element.31, f32[64]{0:T(128)S(1)} %get-tuple-element.19, ...), kind=kLoop, calls=%fused_computation.5 | loop fusion | flops 4194304 | bytes 4195584 | tf_op jit(solution)/shard_map/convert_element_type | solution.py:51
  86.4 1.8 %fusion.52 = f32[32,256,64]{1,2,0:T(8,128)} fusion(bf16[1,64,32,256]{3,1,2,0:T(8,128)(2,1)S(1)} %fusion.2, bf16[3,3,64,64]{3,2,1,0:T(8,128)(2,1)S(1)} %copy-done.18), kind=kOutput, calls=%fused_computation.89 | convolution fusion | flops 67108864 | bytes 3162112 | tf_op jit(solution)/shard_map/oc,bohw->bchw/dot_general | solution.py:60
  91.2 1.3 fusion.11
  96.3 4.5 %collective-permute-start.4 = (bf16[1,64,1,256]{3,1,2,0:T(8,128)(2,1)S(1)}, bf16[1,64,1,256]{3,1,2,0:T(8,128)(2,1)S(1)}, u32[]{:S(2)}, u32[]{:S(2)}) collective-permute-start(bf16[1,64,1,256]{3,1,2,0:T(8,128)(2,1)S(1)} %get-tuple-element.28), channel_id=1, source_target_pairs={{0,2},{2,4},{4,6},{1,3},{3,5},{5,7},{8,10},{10,12},{12,14},{9,11},... | collective-permute-start | bytes 98312 | tf_op jit(solution)/shard_map/ppermute | solution.py:14
  104.8 3.2 %collective-permute-start.7 = (bf16[1,64,34,1]{1,2,3,0:T(8,128)(2,1)S(1)}, bf16[1,64,34,1]{1,2,3,0:T(8,128)(2,1)S(1)}, u32[]{:S(2)}, u32[]{:S(2)}) collective-permute-start(bf16[1,64,34,1]{1,2,3,0:T(8,128)(2,1)S(1)} %copy.41), channel_id=1, source_target_pairs={{0,1},{2,3},{4,5},{6,7},{8,9},{10,11},{12,13},{14,15},{16,17},{18,... | collective-permute-start | bytes 13064 | tf_op jit(solution)/shard_map/ppermute | solution.py:14
  108.1 1.8 %fusion.35 = f32[32,256,64]{1,2,0:T(8,128)} fusion(bf16[1,64,1,256]{3,1,2,0:T(8,128)(2,1)S(1)} %collective-permute-done.5, bf16[1,64,32,256]{3,1,2,0:T(8,128)(2,1)S(1)} %fusion.2, bf16[3,3,64,64]{3,2,1,0:T(8,128)(2,1)S(1)} %copy-done.18), kind=kOutput, calls=%fused_computation.68 | convolution fusion | flops 67633152 | bytes 3194880 | tf_op jit(solution)/shard_map/oc,bohw->bchw/dot_general | solution.py:60
  109.9 1.8 %fusion.27 = f32[32,256,64]{1,2,0:T(8,128)} fusion(bf16[1,64,32,256]{3,1,2,0:T(8,128)(2,1)S(1)} %fusion.2, bf16[1,64,1,256]{3,1,2,0:T(8,128)(2,1)S(1)} %collective-permute-done.4, bf16[3,3,64,64]{3,2,1,0:T(8,128)(2,1)S(1)} %copy-done.18), kind=kOutput, calls=%fused_computation.56 | convolution fusion | flops 67633152 | bytes 3194880 | tf_op jit(solution)/shard_map/oc,bohw->bchw/dot_general | solution.py:60
  112.5 1.4 maximum_maximum_fusion
  118.5 1.6 fusion.24
  120.1 1.6 copy.51
  121.6 3.8 %reduce-scatter.2.cloned.1.call-done = f32[3,3,16,64]{3,2,1,0:T(8,128)} async-done(((f32[3,3,64,64]{3,2,1,0:T(8,128)}), f32[3,3,16,64]{3,2,1,0:T(8,128)}) %reduce-scatter.2.cloned.1.call-update) | async-done | bytes 36880 | tf_op jit(solution)/shard_map/reduce_scatter | solution.py:73
  125.5 30.0 %psum.40 = f32[3,3,16,64]{3,2,1,0:T(8,128)} all-reduce(f32[3,3,16,64]{3,2,1,0:T(8,128)} %reduce-scatter.2.cloned.1.call-done), channel_id=1, replica_groups=mesh['dp'=4,'row'=4,'col'=2] {'row','col'}, use_global_device_ids=true, to_apply=%region_8.0 | all-reduce | flops 9216 | bytes 73728 | tf_op jit(solution)/shard_map/psum | solution.py:72
  (92 shorter events, 24.9 us)
Async XLA Ops:
  7.2 8.3 %copy-start.8 = (bf16[1,64,32,256]{3,2,1,0:T(8,128)(2,1)S(1)}, bf16[1,64,32,256]{3,2,1,0:T(8,128)(2,1)}, u32[]{:S(2)}) copy-start(bf16[1,64,32,256]{3,2,1,0:T(8,128)(2,1)} %param.4) | copy-start | bytes 3145732
  7.2 8.3 %copy-start.18 = (bf16[3,3,64,64]{3,2,1,0:T(8,128)(2,1)S(1)}, bf16[3,3,64,64]{3,2,1,0:T(8,128)(2,1)}, u32[]{:S(2)}) copy-start(bf16[3,3,64,64]{3,2,1,0:T(8,128)(2,1)} %param.5) | copy-start | bytes 221188
  7.2 118.3 %reduce-scatter.2.cloned.1.call-start = ((), (), s32[]{:S(2)}) async-start(), calls=%async_computation.1 | async-start | bytes 368640 | tf_op jit(solution)/shard_map/reduce_scatter | solution.py:73
  9.1 17.8 %copy-start.6 = (bf16[1,64,32,256]{3,1,2,0:T(8,128)(2,1)}, bf16[1,64,32,256]{3,1,2,0:T(8,128)(2,1)S(1)}, u32[]{:S(2)}) copy-start(bf16[1,64,32,256]{3,1,2,0:T(8,128)(2,1)S(1)} %copy.26) | copy-start | bytes 3145732
  9.2 8.5 %collective-permute-start = (bf16[1,64,1,256]{3,1,2,0:T(8,128)(2,1)S(1)}, bf16[1,64,1,256]{3,1,2,0:T(8,128)(2,1)S(1)}, u32[]{:S(2)}, u32[]{:S(2)}) collective-permute-start(bf16[1,64,1,256]{3,1,2,0:T(8,128)(2,1)S(1)} %get-tuple-element.29), channel_id=1, source_target_pairs={{0,2},{2,4},{4,6},{1,3},{3,5},{5,7},{8,10},{10,12},{12,14},{9,11},... | collective-permute-start | bytes 98312 | tf_op jit(solution)/shard_map/ppermute | solution.py:14
  14.1 5.8 %collective-permute-start.1 = (bf16[1,64,1,256]{3,1,2,0:T(8,128)(2,1)S(1)}, bf16[1,64,1,256]{3,1,2,0:T(8,128)(2,1)S(1)}, u32[]{:S(2)}, u32[]{:S(2)}) collective-permute-start(bf16[1,64,1,256]{3,1,2,0:T(8,128)(2,1)S(1)} %get-tuple-element.30), channel_id=1, source_target_pairs={{2,0},{4,2},{6,4},{3,1},{5,3},{7,5},{10,8},{12,10},{14,12},{11,9},... | collective-permute-start | bytes 98312 | tf_op jit(solution)/shard_map/ppermute | solution.py:15
  20.6 8.1 %collective-permute-start.3 = (bf16[1,64,34,1]{1,2,3,0:T(8,128)(2,1)S(1)}, bf16[1,64,34,1]{1,2,3,0:T(8,128)(2,1)S(1)}, u32[]{:S(2)}, u32[]{:S(2)}) collective-permute-start(bf16[1,64,34,1]{1,2,3,0:T(8,128)(2,1)S(1)} %copy.32), channel_id=1, source_target_pairs={{1,0},{3,2},{5,4},{7,6},{9,8},{11,10},{13,12},{15,14},{17,16},{19,... | collective-permute-start | bytes 13064 | tf_op jit(solution)/shard_map/ppermute | solution.py:15
  22.2 11.0 %collective-permute-start.2 = (bf16[1,64,34,1]{1,2,3,0:T(8,128)(2,1)S(1)}, bf16[1,64,34,1]{1,2,3,0:T(8,128)(2,1)S(1)}, u32[]{:S(2)}, u32[]{:S(2)}) collective-permute-start(bf16[1,64,34,1]{1,2,3,0:T(8,128)(2,1)S(1)} %copy.29), channel_id=1, source_target_pairs={{0,1},{2,3},{4,5},{6,7},{8,9},{10,11},{12,13},{14,15},{16,17},{18,... | collective-permute-start | bytes 13064 | tf_op jit(solution)/shard_map/ppermute | solution.py:14
  29.1 4.2 %copy-start.1 = (bf16[1,64,34,1]{3,1,2,0:T(8,128)(2,1)}, bf16[1,64,34,1]{3,1,2,0:T(8,128)(2,1)S(1)}, u32[]{:S(2)}) copy-start(bf16[1,64,34,1]{3,1,2,0:T(8,128)(2,1)S(1)} %copy.33) | copy-start | bytes 13060
  33.6 2.4 %copy-start.17 = (f32[32,256,64]{1,2,0:T(8,128)S(1)}, f32[32,256,64]{1,2,0:T(8,128)}, u32[]{:S(2)}) copy-start(f32[32,256,64]{1,2,0:T(8,128)} %fusion.86) | copy-start | bytes 6291460
  34.2 2.6 %copy-start.14 = (f32[32,256,64]{1,2,0:T(8,128)S(1)}, f32[32,256,64]{1,2,0:T(8,128)}, u32[]{:S(2)}) copy-start(f32[32,256,64]{1,2,0:T(8,128)} %fusion.58) | copy-start | bytes 6291460
  34.2 3.2 %copy-start.15 = (f32[32,256,64]{1,2,0:T(8,128)S(1)}, f32[32,256,64]{1,2,0:T(8,128)}, u32[]{:S(2)}) copy-start(f32[32,256,64]{1,2,0:T(8,128)} %fusion.61) | copy-start | bytes 6291460
  34.8 2.7 %copy-start.2 = (bf16[1,64,34,1]{3,1,2,0:T(8,128)(2,1)S(1)}, bf16[1,64,34,1]{3,1,2,0:T(8,128)(2,1)}, u32[]{:S(2)}) copy-start(bf16[1,64,34,1]{3,1,2,0:T(8,128)(2,1)} %copy-done.1) | copy-start | bytes 13060
  34.8 3.5 %copy-start.11 = (f32[32,256,64]{1,2,0:T(8,128)S(1)}, f32[32,256,64]{1,2,0:T(8,128)}, u32[]{:S(2)}) copy-start(f32[32,256,64]{1,2,0:T(8,128)} %fusion.55) | copy-start | bytes 6291460
  42.1 40.9 %copy-start = (f32[32,256,64]{1,2,0:T(8,128)}, f32[32,256,64]{1,2,0:T(8,128)S(1)}, u32[]{:S(2)}) copy-start(f32[32,256,64]{1,2,0:T(8,128)S(1)} %get-tuple-element.34) | copy-start | bytes 6291460
  42.1 40.9 %copy-start.21 = (f32[64]{0:T(128)S(1)}, f32[64]{0:T(128)}, u32[]{:S(2)}) copy-start(f32[64]{0:T(128)} %param.6) | copy-start | bytes 772
  83.0 2.8 %copy-start.19 = (f32[64]{0:T(128)}, f32[64]{0:T(128)S(1)}, u32[]{:S(2)}) copy-start(f32[64]{0:T(128)S(1)} %get-tuple-element.31) | copy-start | bytes 772
  83.0 2.8 %copy-start.20 = (f32[64]{0:T(128)}, f32[64]{0:T(128)S(1)}, u32[]{:S(2)}) copy-start(f32[64]{0:T(128)S(1)} %get-tuple-element.32) | copy-start | bytes 772
  83.0 2.8 %copy-start.5 = (bf16[1,64,34,1]{3,1,2,0:T(8,128)(2,1)S(1)}, bf16[1,64,34,1]{3,1,2,0:T(8,128)(2,1)}, u32[]{:S(2)}) copy-start(bf16[1,64,34,1]{3,1,2,0:T(8,128)(2,1)} %copy-done.4) | copy-start | bytes 13060
  95.0 6.6 %collective-permute-start.5 = (bf16[1,64,1,256]{3,1,2,0:T(8,128)(2,1)S(1)}, bf16[1,64,1,256]{3,1,2,0:T(8,128)(2,1)S(1)}, u32[]{:S(2)}, u32[]{:S(2)}) collective-permute-start(bf16[1,64,1,256]{3,1,2,0:T(8,128)(2,1)S(1)} %get-tuple-element.27), channel_id=1, source_target_pairs={{2,0},{4,2},{6,4},{3,1},{5,3},{7,5},{10,8},{12,10},{14,12},{11,9},... | collective-permute-start | bytes 98312 | tf_op jit(solution)/shard_map/ppermute | solution.py:15
  96.3 6.1 %collective-permute-start.4 = (bf16[1,64,1,256]{3,1,2,0:T(8,128)(2,1)S(1)}, bf16[1,64,1,256]{3,1,2,0:T(8,128)(2,1)S(1)}, u32[]{:S(2)}, u32[]{:S(2)}) collective-permute-start(bf16[1,64,1,256]{3,1,2,0:T(8,128)(2,1)S(1)} %get-tuple-element.28), channel_id=1, source_target_pairs={{0,2},{2,4},{4,6},{1,3},{3,5},{5,7},{8,10},{10,12},{12,14},{9,11},... | collective-permute-start | bytes 98312 | tf_op jit(solution)/shard_map/ppermute | solution.py:14
  103.2 8.5 %collective-permute-start.6 = (bf16[1,64,34,1]{1,2,3,0:T(8,128)(2,1)S(1)}, bf16[1,64,34,1]{1,2,3,0:T(8,128)(2,1)S(1)}, u32[]{:S(2)}, u32[]{:S(2)}) collective-permute-start(bf16[1,64,34,1]{1,2,3,0:T(8,128)(2,1)S(1)} %copy.37), channel_id=1, source_target_pairs={{1,0},{3,2},{5,4},{7,6},{9,8},{11,10},{13,12},{15,14},{17,16},{19,... | collective-permute-start | bytes 13064 | tf_op jit(solution)/shard_map/ppermute | solution.py:15
  104.8 7.3 %collective-permute-start.7 = (bf16[1,64,34,1]{1,2,3,0:T(8,128)(2,1)S(1)}, bf16[1,64,34,1]{1,2,3,0:T(8,128)(2,1)S(1)}, u32[]{:S(2)}, u32[]{:S(2)}) collective-permute-start(bf16[1,64,34,1]{1,2,3,0:T(8,128)(2,1)S(1)} %copy.41), channel_id=1, source_target_pairs={{0,1},{2,3},{4,5},{6,7},{8,9},{10,11},{12,13},{14,15},{16,17},{18,... | collective-permute-start | bytes 13064 | tf_op jit(solution)/shard_map/ppermute | solution.py:14
  116.0 2.5 %copy-start.10 = (f32[32,256,64]{1,2,0:T(8,128)S(1)}, f32[32,256,64]{1,2,0:T(8,128)}, u32[]{:S(2)}) copy-start(f32[32,256,64]{1,2,0:T(8,128)} %fusion.52) | copy-start | bytes 6291460
  (7 other events, 10.9 us)
Sparse Core Ops, SparseCore 0:
  101.8 23.6 reduce-scatter.1
where the time goes:
time: 163 us; the launch traced here: 162 us
  blocking collectives  70.7 us (43%)
  matrix products  31.1 us (19%)
  starting transfers between devices  21 us (13%)
  between operations  14.6 us (9%)
  local copies, waits for them, and re-layouts  13.5 us (8%)
  waiting for transfers between devices  6.31 us (4%)
  other arithmetic  5.31 us (3%)
    psum x1, blocking collectives, per_device(): lax.psum((local_pre, local_sq, local_cot, local_cross), ('dp', 'row', 'co...  40.6 us
    psum x1, blocking collectives, per_device(): spatial = lax.psum(local_kernel, ('row', 'col'))  30 us
    ppermute x4, starting transfers between devices, with_halo(): before = lax.ppermute(last, axis, up)  15.8 us
    dot_general x9, matrix products, per_device(): jnp.einsum('oc,bchw->bohw', kernel[tap_row, tap_col], window, preferred_e...  15.4 us
    unnamed x48, local copies, waits for them, and re-layouts  10.1 us
    dot_general x9, matrix products, per_device(): jnp.einsum('oc,bohw->bchw', kernel[tap_row, tap_col], shifted, preferred_...  9.7 us
    dot_general x9, matrix products, per_device(): jnp.einsum('bohw,bchw->oc', pre_grad, window, preferred_element_type=jnp....  5.99 us
    ppermute x4, starting transfers between devices, with_halo(): after = lax.ppermute(initial, axis, down)  5.16 us
  transfers between devices with their start and end apart: 9, of which 3 were waited for; matrix products, arithmetic and copies ran while one was open for 15% of the time, Pallas kernels for 0%

commit v1 on v0

--- a/solution.py
+++ b/solution.py
@@ -69,7 +69,7 @@
             )
     factor = total ** (-0.5)
     local_kernel = jnp.stack(kernel_terms).reshape(3, 3, channels, channels) * factor
-    spatial = lax.psum(local_kernel, ("row", "col"))
+    spatial = lax.psum(lax.psum(local_kernel, "row"), "col")
     weight_grad = lax.psum_scatter(spatial, "dp", scatter_dimension=2, tiled=True)
     return (input_grad.astype(jnp.bfloat16), weight_grad, sum_norm / total, sum_cot / total)
 

time: 163 us -> 158 us (0.969)
  blocking collectives: 70.7 us -> 65.2 us
    psum x1 -> x2, blocking collectives: 30 us -> 24.6 us  [per_device(): spatial = lax.psum(lax.psum(local_kernel, 'row'), 'col')]
  transfers between devices with their start and end apart: 9 -> 9, of which waited for: 3 -> 3; matrix products, arithmetic and copies ran while one was open for 15% -> 16% of each run, Pallas kernels for 0% -> 0%
where the time goes in v1:
time: 158 us; the launch traced here: 157 us
  blocking collectives  65.2 us (41%)
  matrix products  31.1 us (20%)
  starting transfers between devices  21 us (13%)
  between operations  14.6 us (9%)
  local copies, waits for them, and re-layouts  13.5 us (9%)
  waiting for transfers between devices  6.3 us (4%)
  other arithmetic  5.31 us (3%)
    psum x1, blocking collectives, per_device(): lax.psum((local_pre, local_sq, local_cot, local_cross), ('dp', 'row', 'co...  40.6 us
    psum x2, blocking collectives, per_device(): spatial = lax.psum(lax.psum(local_kernel, 'row'), 'col')  24.6 us
    ppermute x4, starting transfers between devices, with_halo(): before = lax.ppermute(last, axis, up)  15.8 us
    dot_general x9, matrix products, per_device(): jnp.einsum('oc,bchw->bohw', kernel[tap_row, tap_col], window, preferred_e...  15.4 us
    unnamed x48, local copies, waits for them, and re-layouts  10.1 us
    dot_general x9, matrix products, per_device(): jnp.einsum('oc,bohw->bchw', kernel[tap_row, tap_col], shifted, preferred_...  9.75 us
    dot_general x9, matrix products, per_device(): jnp.einsum('bohw,bchw->oc', pre_grad, window, preferred_element_type=jnp....  5.99 us
    ppermute x4, starting transfers between devices, with_halo(): after = lax.ppermute(initial, axis, down)  5.16 us
  transfers between devices with their start and end apart: 9, of which 3 were waited for; matrix products, arithmetic and copies ran while one was open for 16% of the time, Pallas kernels for 0%

profile of v1, /device:TPU:0, one launch (start us, length us, event | category | flops | bytes accessed | tf_op | source)
XLA Modules:
  0.0 157.0 jit_solution(7941235415792395592)
XLA Ops:
  7.2 1.9 %copy.26 = bf16[1,64,32,256]{3,1,2,0:T(8,128)(2,1)S(1)} copy(bf16[1,64,32,256]{3,2,1,0:T(8,128)(2,1)} %param.4) | data formatting | bytes 2097152 | tf_op args[0]
  9.2 5.0 %collective-permute-start = (bf16[1,64,1,256]{3,1,2,0:T(8,128)(2,1)S(1)}, bf16[1,64,1,256]{3,1,2,0:T(8,128)(2,1)S(1)}, u32[]{:S(2)}, u32[]{:S(2)}) collective-permute-start(bf16[1,64,1,256]{3,1,2,0:T(8,128)(2,1)S(1)} %get-tuple-element.29), channel_id=1, source_target_pairs={{0,2},{2,4},{4,6},{1,3},{3,5},{5,7},{8,10},{10,12},{12,14},{9,11},... | collective-permute-start | bytes 98312 | tf_op jit(solution)/shard_map/ppermute | solution.py:14
  15.4 2.2 %fusion.55 = f32[32,256,64]{1,2,0:T(8,128)} fusion(bf16[64,32,256]{2,1,0:T(8,128)(2,1)S(1)} %bitcast.222, bf16[3,3,64,64]{3,2,1,0:T(8,128)(2,1)S(1)} %copy-done.18), kind=kOutput, calls=%fused_computation.92 | convolution fusion | flops 67108864 | bytes 3162112 | tf_op jit(solution)/shard_map/oc,bchw->bohw/dot_general | solution.py:30
  18.3 1.7 %collective-permute-done.1 = bf16[1,64,1,256]{3,1,2,0:T(8,128)(2,1)S(1)} collective-permute-done((bf16[1,64,1,256]{3,1,2,0:T(8,128)(2,1)S(1)}, bf16[1,64,1,256]{3,1,2,0:T(8,128)(2,1)S(1)}, u32[]{:S(2)}, u32[]{:S(2)}) %collective-permute-start.1) | collective-permute-done | bytes 32800 | tf_op jit(solution)/shard_map/ppermute | solution.py:15
  22.2 3.0 %collective-permute-start.2 = (bf16[1,64,34,1]{1,2,3,0:T(8,128)(2,1)S(1)}, bf16[1,64,34,1]{1,2,3,0:T(8,128)(2,1)S(1)}, u32[]{:S(2)}, u32[]{:S(2)}) collective-permute-start(bf16[1,64,34,1]{1,2,3,0:T(8,128)(2,1)S(1)} %copy.29), channel_id=1, source_target_pairs={{0,1},{2,3},{4,5},{6,7},{8,9},{10,11},{12,13},{14,15},{16,17},{18,... | collective-permute-start | bytes 13064 | tf_op jit(solution)/shard_map/ppermute | solution.py:14
  25.2 1.8 %fusion.58 = f32[32,256,64]{1,2,0:T(8,128)} fusion(bf16[1,64,32,256]{3,1,2,0:T(8,128)(2,1)S(1)} %copy.26, bf16[1,64,1,256]{3,1,2,0:T(8,128)(2,1)S(1)} %collective-permute-done, bf16[3,3,64,64]{3,2,1,0:T(8,128)(2,1)S(1)} %copy-done.18), kind=kOutput, calls=%fused_computation.94 | convolution fusion | flops 69206016 | bytes 3194880 | tf_op jit(solution)/shard_map/oc,bchw->bohw/dot_general | solution.py:30
  27.0 1.7 %fusion.61 = f32[32,256,64]{1,2,0:T(8,128)} fusion(bf16[1,64,1,256]{3,1,2,0:T(8,128)(2,1)S(1)} %collective-permute-done.1, bf16[1,64,32,256]{3,1,2,0:T(8,128)(2,1)S(1)} %copy.26, bf16[3,3,64,64]{3,2,1,0:T(8,128)(2,1)S(1)} %copy-done.18), kind=kOutput, calls=%fused_computation.95 | convolution fusion | flops 69206016 | bytes 3194880 | tf_op jit(solution)/shard_map/oc,bchw->bohw/dot_general | solution.py:30
  29.1 2.0 %fusion.78 = f32[32,256,64]{1,2,0:T(8,128)} fusion(bf16[3,3,64,64]{3,2,1,0:T(8,128)(2,1)S(1)} %copy-done.18, bf16[1,64,34,256]{3,1,2,0:T(8,128)(2,1)S(1)} %constant_dynamic-update-slice_fusion, bf16[1,64,34,1]{3,1,2,0:T(8,128)(2,1)S(1)} %copy.33), kind=kOutput, calls=%fused_computation.109 | convolution fusion | flops 69206016 | bytes 3784704 | tf_op jit(solution)/shard_map/oc,bchw->bohw/dot_general | solution.py:30
  31.1 2.1 %fusion.86 = f32[32,256,64]{1,2,0:T(8,128)} fusion(bf16[3,3,64,64]{3,2,1,0:T(8,128)(2,1)S(1)} %copy-done.18, bf16[1,64,34,256]{3,1,2,0:T(8,128)(2,1)S(1)} %constant_dynamic-update-slice_fusion, bf16[1,64,34,1]{3,1,2,0:T(8,128)(2,1)S(1)} %copy.33), kind=kOutput, calls=%fused_computation.117 | convolution fusion | flops 69206016 | bytes 3784704 | tf_op jit(solution)/shard_map/oc,bchw->bohw/dot_general | solution.py:30
  38.3 3.8 %fusion.3 = (f32[64]{0:T(128)S(1)}, f32[64]{0:T(128)S(1)}, f32[64]{0:T(128)S(1)}, f32[32,256,64]{1,2,0:T(8,128)S(1)}) fusion(bf16[1,64,32,256]{3,2,1,0:T(8,128)(2,1)} %param.7, bf16[1,64,34,1]{3,1,2,0:T(8,128)(2,1)S(1)} %copy-done.2, bf16[1,64,34,256]{3,1,2,0:T(8,128)(2,1)S(1)} %constant_dynamic-update-slice_fusion, ...), kind=kOutput, calls=%fused_computation.6 | convolution fusion | flops 76545856 | bytes 21611264 | tf_op jit(solution)/shard_map/oc,bchw->bohw/dot_general | solution.py:30
  42.4 40.6 %all-reduce = (f32[64]{0:T(128)S(1)}, f32[64]{0:T(128)S(1)}, f32[64]{0:T(128)S(1)}, f32[64]{0:T(128)S(1)}) all-reduce(f32[64]{0:T(128)S(1)} %get-tuple-element.13, f32[64]{0:T(128)S(1)} %reduce_sum.37, f32[64]{0:T(128)S(1)} %get-tuple-element.12, f32[64]{0:T(128)S(1)} %get-tuple-element.14), channel_id=1, replica_groups=mesh['dp'=4,'row'=4,'col'=2] {'dp','row','col'}, use_global_device_ids=true, to_apply=%region_1.0 | all-reduce | flops 256 | bytes 2048 | tf_op jit(solution)/shard_map/psum | solution.py:41
  83.1 2.8 %fusion.2 = bf16[1,64,32,256]{3,1,2,0:T(8,128)(2,1)S(1)} fusion(f32[32,256,64]{1,2,0:T(8,128)} %copy-done, f32[64]{0:T(128)S(1)} %get-tuple-element.32, f32[64]{0:T(128)S(1)} %get-tuple-element.20, f32[64]{0:T(128)S(1)} %get-tuple-element.33, f32[64]{0:T(128)S(1)} %get-tuple-element.31, f32[64]{0:T(128)S(1)} %get-tuple-element.19, ...), kind=kLoop, calls=%fused_computation.5 | loop fusion | flops 4194304 | bytes 4195584 | tf_op jit(solution)/shard_map/convert_element_type | solution.py:51
  86.5 1.8 %fusion.52 = f32[32,256,64]{1,2,0:T(8,128)} fusion(bf16[1,64,32,256]{3,1,2,0:T(8,128)(2,1)S(1)} %fusion.2, bf16[3,3,64,64]{3,2,1,0:T(8,128)(2,1)S(1)} %copy-done.18), kind=kOutput, calls=%fused_computation.89 | convolution fusion | flops 67108864 | bytes 3162112 | tf_op jit(solution)/shard_map/oc,bohw->bchw/dot_general | solution.py:60
  91.3 1.3 fusion.11
  96.3 4.5 %collective-permute-start.4 = (bf16[1,64,1,256]{3,1,2,0:T(8,128)(2,1)S(1)}, bf16[1,64,1,256]{3,1,2,0:T(8,128)(2,1)S(1)}, u32[]{:S(2)}, u32[]{:S(2)}) collective-permute-start(bf16[1,64,1,256]{3,1,2,0:T(8,128)(2,1)S(1)} %get-tuple-element.28), channel_id=1, source_target_pairs={{0,2},{2,4},{4,6},{1,3},{3,5},{5,7},{8,10},{10,12},{12,14},{9,11},... | collective-permute-start | bytes 98312 | tf_op jit(solution)/shard_map/ppermute | solution.py:14
  104.8 3.2 %collective-permute-start.7 = (bf16[1,64,34,1]{1,2,3,0:T(8,128)(2,1)S(1)}, bf16[1,64,34,1]{1,2,3,0:T(8,128)(2,1)S(1)}, u32[]{:S(2)}, u32[]{:S(2)}) collective-permute-start(bf16[1,64,34,1]{1,2,3,0:T(8,128)(2,1)S(1)} %copy.41), channel_id=1, source_target_pairs={{0,1},{2,3},{4,5},{6,7},{8,9},{10,11},{12,13},{14,15},{16,17},{18,... | collective-permute-start | bytes 13064 | tf_op jit(solution)/shard_map/ppermute | solution.py:14
  108.1 1.9 %fusion.35 = f32[32,256,64]{1,2,0:T(8,128)} fusion(bf16[1,64,1,256]{3,1,2,0:T(8,128)(2,1)S(1)} %collective-permute-done.5, bf16[1,64,32,256]{3,1,2,0:T(8,128)(2,1)S(1)} %fusion.2, bf16[3,3,64,64]{3,2,1,0:T(8,128)(2,1)S(1)} %copy-done.18), kind=kOutput, calls=%fused_computation.68 | convolution fusion | flops 67633152 | bytes 3194880 | tf_op jit(solution)/shard_map/oc,bohw->bchw/dot_general | solution.py:60
  109.9 1.8 %fusion.27 = f32[32,256,64]{1,2,0:T(8,128)} fusion(bf16[1,64,32,256]{3,1,2,0:T(8,128)(2,1)S(1)} %fusion.2, bf16[1,64,1,256]{3,1,2,0:T(8,128)(2,1)S(1)} %collective-permute-done.4, bf16[3,3,64,64]{3,2,1,0:T(8,128)(2,1)S(1)} %copy-done.18), kind=kOutput, calls=%fused_computation.56 | convolution fusion | flops 67633152 | bytes 3194880 | tf_op jit(solution)/shard_map/oc,bohw->bchw/dot_general | solution.py:60
  112.5 1.4 maximum_maximum_fusion
  118.5 1.6 %fusion.24 = bf16[1,64,32,256]{3,1,2,0:T(8,128)(2,1)S(1)} fusion(f32[32,256,64]{1,2,0:T(8,128)S(1)} %copy-done.13, f32[32,256,64]{1,2,0:T(8,128)S(1)} %fusion.30, f32[32,256,64]{1,2,0:T(8,128)S(1)} %fusion.31, f32[32,256,64]{1,2,0:T(8,128)S(1)} %copy-done.10, f32[32,256,64]{1,2,0:T(8,128)S(1)} %fusion.32, f32[32,256,64]{1,2,0:T(8,128)S(1)} %fusion.33, ...), kind=kOutput, calls=%fused_computation.51 | convolution fusion | flops 71827456 | bytes 18890752 | tf_op jit(solution)/shard_map/oc,bohw->bchw/dot_general | solution.py:60
  120.1 1.6 copy.51
  121.7 3.8 %reduce-scatter.2.cloned.1.call-done = f32[3,3,16,64]{3,2,1,0:T(8,128)} async-done(((f32[3,3,64,64]{3,2,1,0:T(8,128)}), f32[3,3,16,64]{3,2,1,0:T(8,128)}) %reduce-scatter.2.cloned.1.call-update) | async-done | bytes 36880 | tf_op jit(solution)/shard_map/reduce_scatter | solution.py:73
  125.5 20.5 %psum.49 = f32[3,3,16,64]{3,2,1,0:T(8,128)S(1)} all-reduce(f32[3,3,16,64]{3,2,1,0:T(8,128)} %reduce-scatter.2.cloned.1.call-done), channel_id=1, replica_groups=mesh['dp'=4,'row'=4,'col'=2] {'row'}, use_global_device_ids=true, to_apply=%region_8.0 | all-reduce | flops 9216 | bytes 73728 | tf_op jit(solution)/shard_map/psum | solution.py:72
  146.0 4.1 %psum.48 = f32[3,3,16,64]{3,2,1,0:T(8,128)} all-reduce(f32[3,3,16,64]{3,2,1,0:T(8,128)S(1)} %psum.49), channel_id=1, replica_groups=mesh['dp'=4,'row'=4,'col'=2] {'col'}, use_global_device_ids=true, to_apply=%region_9.0 | all-reduce | flops 9216 | bytes 73728 | tf_op jit(solution)/shard_map/psum | solution.py:72
  (93 shorter events, 26.2 us)
Async XLA Ops:
  7.2 8.3 %copy-start.8 = (bf16[1,64,32,256]{3,2,1,0:T(8,128)(2,1)S(1)}, bf16[1,64,32,256]{3,2,1,0:T(8,128)(2,1)}, u32[]{:S(2)}) copy-start(bf16[1,64,32,256]{3,2,1,0:T(8,128)(2,1)} %param.4) | copy-start | bytes 3145732
  7.2 8.3 %copy-start.18 = (bf16[3,3,64,64]{3,2,1,0:T(8,128)(2,1)S(1)}, bf16[3,3,64,64]{3,2,1,0:T(8,128)(2,1)}, u32[]{:S(2)}) copy-start(bf16[3,3,64,64]{3,2,1,0:T(8,128)(2,1)} %param.5) | copy-start | bytes 221188
  7.2 118.3 %reduce-scatter.2.cloned.1.call-start = ((), (), s32[]{:S(2)}) async-start(), calls=%async_computation.1 | async-start | bytes 368640 | tf_op jit(solution)/shard_map/reduce_scatter | solution.py:73
  9.1 17.8 %copy-start.6 = (bf16[1,64,32,256]{3,1,2,0:T(8,128)(2,1)}, bf16[1,64,32,256]{3,1,2,0:T(8,128)(2,1)S(1)}, u32[]{:S(2)}) copy-start(bf16[1,64,32,256]{3,1,2,0:T(8,128)(2,1)S(1)} %copy.26) | copy-start | bytes 3145732
  9.2 8.5 %collective-permute-start = (bf16[1,64,1,256]{3,1,2,0:T(8,128)(2,1)S(1)}, bf16[1,64,1,256]{3,1,2,0:T(8,128)(2,1)S(1)}, u32[]{:S(2)}, u32[]{:S(2)}) collective-permute-start(bf16[1,64,1,256]{3,1,2,0:T(8,128)(2,1)S(1)} %get-tuple-element.29), channel_id=1, source_target_pairs={{0,2},{2,4},{4,6},{1,3},{3,5},{5,7},{8,10},{10,12},{12,14},{9,11},... | collective-permute-start | bytes 98312 | tf_op jit(solution)/shard_map/ppermute | solution.py:14
  14.1 5.8 %collective-permute-start.1 = (bf16[1,64,1,256]{3,1,2,0:T(8,128)(2,1)S(1)}, bf16[1,64,1,256]{3,1,2,0:T(8,128)(2,1)S(1)}, u32[]{:S(2)}, u32[]{:S(2)}) collective-permute-start(bf16[1,64,1,256]{3,1,2,0:T(8,128)(2,1)S(1)} %get-tuple-element.30), channel_id=1, source_target_pairs={{2,0},{4,2},{6,4},{3,1},{5,3},{7,5},{10,8},{12,10},{14,12},{11,9},... | collective-permute-start | bytes 98312 | tf_op jit(solution)/shard_map/ppermute | solution.py:15
  20.6 8.2 %collective-permute-start.3 = (bf16[1,64,34,1]{1,2,3,0:T(8,128)(2,1)S(1)}, bf16[1,64,34,1]{1,2,3,0:T(8,128)(2,1)S(1)}, u32[]{:S(2)}, u32[]{:S(2)}) collective-permute-start(bf16[1,64,34,1]{1,2,3,0:T(8,128)(2,1)S(1)} %copy.32), channel_id=1, source_target_pairs={{1,0},{3,2},{5,4},{7,6},{9,8},{11,10},{13,12},{15,14},{17,16},{19,... | collective-permute-start | bytes 13064 | tf_op jit(solution)/shard_map/ppermute | solution.py:15
  22.2 11.1 %collective-permute-start.2 = (bf16[1,64,34,1]{1,2,3,0:T(8,128)(2,1)S(1)}, bf16[1,64,34,1]{1,2,3,0:T(8,128)(2,1)S(1)}, u32[]{:S(2)}, u32[]{:S(2)}) collective-permute-start(bf16[1,64,34,1]{1,2,3,0:T(8,128)(2,1)S(1)} %copy.29), channel_id=1, source_target_pairs={{0,1},{2,3},{4,5},{6,7},{8,9},{10,11},{12,13},{14,15},{16,17},{18,... | collective-permute-start | bytes 13064 | tf_op jit(solution)/shard_map/ppermute | solution.py:14
  29.1 4.1 %copy-start.1 = (bf16[1,64,34,1]{3,1,2,0:T(8,128)(2,1)}, bf16[1,64,34,1]{3,1,2,0:T(8,128)(2,1)S(1)}, u32[]{:S(2)}) copy-start(bf16[1,64,34,1]{3,1,2,0:T(8,128)(2,1)S(1)} %copy.33) | copy-start | bytes 13060
  33.6 2.4 %copy-start.17 = (f32[32,256,64]{1,2,0:T(8,128)S(1)}, f32[32,256,64]{1,2,0:T(8,128)}, u32[]{:S(2)}) copy-start(f32[32,256,64]{1,2,0:T(8,128)} %fusion.86) | copy-start | bytes 6291460
  34.2 2.6 %copy-start.14 = (f32[32,256,64]{1,2,0:T(8,128)S(1)}, f32[32,256,64]{1,2,0:T(8,128)}, u32[]{:S(2)}) copy-start(f32[32,256,64]{1,2,0:T(8,128)} %fusion.58) | copy-start | bytes 6291460
  34.2 3.2 %copy-start.15 = (f32[32,256,64]{1,2,0:T(8,128)S(1)}, f32[32,256,64]{1,2,0:T(8,128)}, u32[]{:S(2)}) copy-start(f32[32,256,64]{1,2,0:T(8,128)} %fusion.61) | copy-start | bytes 6291460
  34.8 2.7 %copy-start.2 = (bf16[1,64,34,1]{3,1,2,0:T(8,128)(2,1)S(1)}, bf16[1,64,34,1]{3,1,2,0:T(8,128)(2,1)}, u32[]{:S(2)}) copy-start(bf16[1,64,34,1]{3,1,2,0:T(8,128)(2,1)} %copy-done.1) | copy-start | bytes 13060
  34.8 3.5 %copy-start.11 = (f32[32,256,64]{1,2,0:T(8,128)S(1)}, f32[32,256,64]{1,2,0:T(8,128)}, u32[]{:S(2)}) copy-start(f32[32,256,64]{1,2,0:T(8,128)} %fusion.55) | copy-start | bytes 6291460
  42.1 40.9 %copy-start = (f32[32,256,64]{1,2,0:T(8,128)}, f32[32,256,64]{1,2,0:T(8,128)S(1)}, u32[]{:S(2)}) copy-start(f32[32,256,64]{1,2,0:T(8,128)S(1)} %get-tuple-element.34) | copy-start | bytes 6291460
  42.1 40.9 %copy-start.21 = (f32[64]{0:T(128)S(1)}, f32[64]{0:T(128)}, u32[]{:S(2)}) copy-start(f32[64]{0:T(128)} %param.6) | copy-start | bytes 772
  83.0 2.8 %copy-start.19 = (f32[64]{0:T(128)}, f32[64]{0:T(128)S(1)}, u32[]{:S(2)}) copy-start(f32[64]{0:T(128)S(1)} %get-tuple-element.31) | copy-start | bytes 772
  83.0 2.8 %copy-start.20 = (f32[64]{0:T(128)}, f32[64]{0:T(128)S(1)}, u32[]{:S(2)}) copy-start(f32[64]{0:T(128)S(1)} %get-tuple-element.32) | copy-start | bytes 772
  83.0 2.8 %copy-start.5 = (bf16[1,64,34,1]{3,1,2,0:T(8,128)(2,1)S(1)}, bf16[1,64,34,1]{3,1,2,0:T(8,128)(2,1)}, u32[]{:S(2)}) copy-start(bf16[1,64,34,1]{3,1,2,0:T(8,128)(2,1)} %copy-done.4) | copy-start | bytes 13060
  95.0 6.6 %collective-permute-start.5 = (bf16[1,64,1,256]{3,1,2,0:T(8,128)(2,1)S(1)}, bf16[1,64,1,256]{3,1,2,0:T(8,128)(2,1)S(1)}, u32[]{:S(2)}, u32[]{:S(2)}) collective-permute-start(bf16[1,64,1,256]{3,1,2,0:T(8,128)(2,1)S(1)} %get-tuple-element.27), channel_id=1, source_target_pairs={{2,0},{4,2},{6,4},{3,1},{5,3},{7,5},{10,8},{12,10},{14,12},{11,9},... | collective-permute-start | bytes 98312 | tf_op jit(solution)/shard_map/ppermute | solution.py:15
  96.3 6.1 %collective-permute-start.4 = (bf16[1,64,1,256]{3,1,2,0:T(8,128)(2,1)S(1)}, bf16[1,64,1,256]{3,1,2,0:T(8,128)(2,1)S(1)}, u32[]{:S(2)}, u32[]{:S(2)}) collective-permute-start(bf16[1,64,1,256]{3,1,2,0:T(8,128)(2,1)S(1)} %get-tuple-element.28), channel_id=1, source_target_pairs={{0,2},{2,4},{4,6},{1,3},{3,5},{5,7},{8,10},{10,12},{12,14},{9,11},... | collective-permute-start | bytes 98312 | tf_op jit(solution)/shard_map/ppermute | solution.py:14
  103.2 8.5 %collective-permute-start.6 = (bf16[1,64,34,1]{1,2,3,0:T(8,128)(2,1)S(1)}, bf16[1,64,34,1]{1,2,3,0:T(8,128)(2,1)S(1)}, u32[]{:S(2)}, u32[]{:S(2)}) collective-permute-start(bf16[1,64,34,1]{1,2,3,0:T(8,128)(2,1)S(1)} %copy.37), channel_id=1, source_target_pairs={{1,0},{3,2},{5,4},{7,6},{9,8},{11,10},{13,12},{15,14},{17,16},{19,... | collective-permute-start | bytes 13064 | tf_op jit(solution)/shard_map/ppermute | solution.py:15
  104.8 7.3 %collective-permute-start.7 = (bf16[1,64,34,1]{1,2,3,0:T(8,128)(2,1)S(1)}, bf16[1,64,34,1]{1,2,3,0:T(8,128)(2,1)S(1)}, u32[]{:S(2)}, u32[]{:S(2)}) collective-permute-start(bf16[1,64,34,1]{1,2,3,0:T(8,128)(2,1)S(1)} %copy.41), channel_id=1, source_target_pairs={{0,1},{2,3},{4,5},{6,7},{8,9},{10,11},{12,13},{14,15},{16,17},{18,... | collective-permute-start | bytes 13064 | tf_op jit(solution)/shard_map/ppermute | solution.py:14
  116.1 2.5 %copy-start.10 = (f32[32,256,64]{1,2,0:T(8,128)S(1)}, f32[32,256,64]{1,2,0:T(8,128)}, u32[]{:S(2)}) copy-start(f32[32,256,64]{1,2,0:T(8,128)} %fusion.52) | copy-start | bytes 6291460
  (7 other events, 10.9 us)
Sparse Core Ops, SparseCore 0:
  101.8 23.6 reduce-scatter.1
